TPU v7x, 512 devices: a whole 4x8x8 slice. The times are simulated.
512 devices in a mesh: gx: 4 (over y_lo), gy: 128 (over z, y_hi, x, core).
Axes of the slice: x: 4, y: 8 (y_hi: 2, y_lo: 4; y = y_hi * 4 + y_lo), z: 8, core: 2. Of those that a mesh axis runs over, the one named last changes fastest.
Arguments:
- traces: bfloat16 [8, 256, 128, 256], P('gx', 'gy'), may hold values from -6 to 6
- aperture: int32 [8, 256, 9], P('gx', 'gy'), may hold values 0 or 1
- geometry: int32 [8, 256, 3, 128], P('gx', 'gy'), may hold values from 0 to 1023, as said below
- trace_weight: bfloat16 [8, 256, 128], P('gx', 'gy'), may hold values from 0.0087890625 to 0.03515625
- class_weight: float32 [14], replicated, may hold values from 0.3 to 1.5
- traveltime: int32 [14, 256], replicated, may hold values from 0 to 1114
Outputs:
- image: float32 [64, 1024, 256], P('gx', 'gy')
Inputs may be any that keep to these rules, and one draw needn't show every extreme that they name: Row 0 of a trace's geometry is an inline midpoint among the 16 image columns of its block's tile, row 1 a crossline midpoint among its tile's 8 columns, row 2 an offset class below 8.
All inputs are finite; a program needn't handle non-finite values. No bound on the sum of `aperture` on one device may be relied on, other than what follows from the above.
Results may differ from a plain program's by a relative error of at most 0.0029.
Values may be sent and summed in bfloat16 or wider, within the bound.
A program may use at most 64 MiB of HBM per device.

v0:
```python
import jax
import jax.numpy as jnp
from jax import lax
from jax.sharding import PartitionSpec as P

NS = 256
NTIME = 256
PX = 16
PY = 8
DSTEP = 8


def padded(cells, sides, width):
    for axis, dim in sides:
        count = lax.axis_size(axis)
        ends = count - 1
        head = lax.slice_in_dim(cells, 0, width, axis=dim)
        tail = lax.slice_in_dim(cells, cells.shape[dim] - width, cells.shape[dim], axis=dim)
        cells = jnp.concatenate(
            [
                lax.ppermute(tail, axis, [(i, (i + 1) % count) for i in range(ends)]),
                cells,
                lax.ppermute(head, axis, [((i + 1) % count, i) for i in range(ends)]),
            ],
            axis=dim,
        )
    return cells


def migrate(samples_in, live_weights, geometry, tile_x, tile_y, traveltime, class_weight):
    points = jnp.arange(PX * PY, dtype=jnp.int32)
    point_x = tile_x * PX + points // PY
    point_y = tile_y * PY + points % PY
    distance = jnp.abs(point_x[:, None] - geometry[0][None, :]) + jnp.abs(
        point_y[:, None] - geometry[1][None, :]
    )
    classes = geometry[2][None, :] + distance // DSTEP
    sample_ids = jnp.arange(NS, dtype=jnp.int32)[:, None]

    def add_class(level, image):
        scaled = (live_weights * class_weight[level]).astype(jnp.bfloat16)
        amplitude = jnp.where(classes == level, scaled[None, :], jnp.zeros((), jnp.bfloat16))
        stacked = jnp.dot(amplitude, samples_in, preferred_element_type=jnp.float32)
        quarter = traveltime[level]
        first_sample = quarter // 4
        fraction = (quarter % 4).astype(jnp.float32) * 0.25
        interp = jnp.where(
            sample_ids == first_sample[None, :], 1.0 - fraction[None, :], 0.0
        ) + jnp.where(sample_ids == first_sample[None, :] + 1, fraction[None, :], 0.0)
        return image + jnp.dot(
            stacked, interp, precision=lax.Precision.HIGHEST, preferred_element_type=jnp.float32
        )

    return lax.fori_loop(
        0, class_weight.shape[0], add_class, jnp.zeros((PX * PY, NTIME), jnp.float32)
    )


def per_device(traces, aperture, geometry, trace_weight, class_weight, traveltime):
    blocks = traces.shape[0]
    tile_x = lax.axis_index("gx")
    tile_y = lax.axis_index("gy")
    near_traces, near_weight = (
        padded(traces, (("gx", 0), ("gy", 1)), blocks),
        padded(trace_weight, (("gx", 0), ("gy", 1)), blocks),
    )
    near_aperture, near_geometry = (
        padded(aperture, (("gx", 0), ("gy", 1)), blocks),
        padded(geometry, (("gx", 0), ("gy", 1)), blocks),
    )
    offset = jnp.arange(3 * blocks, dtype=jnp.int32) // blocks - 1
    wanted = (1 - offset)[:, None] * 3 + (1 - offset)[None, :]
    choose = (jnp.arange(9, dtype=jnp.int32)[None, None, :] == wanted[:, :, None]).astype(jnp.int32)
    live_block = jnp.sum(near_aperture * choose, axis=2)
    live = jnp.broadcast_to(live_block[:, :, None], near_weight.shape).reshape(-1)
    live_weights = near_weight.reshape(-1).astype(jnp.float32) * live.astype(jnp.float32)
    flat_geometry = jnp.moveaxis(near_geometry, 2, 0).reshape(3, -1)
    image = migrate(
        near_traces.reshape(-1, NS),
        live_weights,
        flat_geometry,
        tile_x,
        tile_y,
        traveltime,
        class_weight,
    )
    return image.reshape(PX, PY, NTIME)


def solution(mesh):
    return jax.shard_map(
        per_device,
        mesh=mesh,
        in_specs=(
            P("gx", "gy", None, None),
            P("gx", "gy", None),
            P("gx", "gy", None, None),
            P("gx", "gy", None),
            P(),
            P(),
        ),
        out_specs=P("gx", "gy", None),
        check_vma=False,
    )
```

profile of v0, /device:TPU:255, one launch (start us, length us, event | category | flops | bytes accessed | tf_op | source)
XLA Modules:
  0.0 170.8 jit_solution(3702176358756328754)
XLA Ops:
  1.3 4.0 %collective-permute-start.9 = (s32[2,2,9]{2,1,0:T(2,128)}, s32[2,2,9]{2,1,0:T(2,128)S(1)}, u32[]{:S(2)}, u32[]{:S(2)}) collective-permute-start(s32[2,2,9]{2,1,0:T(2,128)} %param.9), channel_id=1, source_target_pairs={{128,0},{256,128},{384,256},{129,1},{257,129},{385,257},{130,2},{2... | collective-permute-start | bytes 440 | tf_op jit(solution)/shard_map/ppermute | solution.py:23
  6.6 4.0 %collective-permute-start.5 = (bf16[2,2,128]{2,1,0:T(2,128)(2,1)}, bf16[2,2,128]{2,1,0:T(2,128)(2,1)S(1)}, u32[]{:S(2)}, u32[]{:S(2)}) collective-permute-start(bf16[2,2,128]{2,1,0:T(2,128)(2,1)} %param.11), channel_id=1, source_target_pairs={{128,0},{256,128},{384,256},{129,1},{257,129},{385,257},{130,2},{2... | collective-permute-start | bytes 3080 | tf_op jit(solution)/shard_map/ppermute | solution.py:23
  12.7 9.0 %collective-permute-start.10 = (s32[6,2,9]{2,1,0:T(2,128)S(1)}, s32[6,2,9]{2,1,0:T(2,128)S(1)}, u32[]{:S(2)}, u32[]{:S(2)}) collective-permute-start(s32[6,2,9]{2,1,0:T(2,128)S(1)} %constant_dynamic-update-slice_fusion.3), channel_id=1, source_target_pairs={{0,1},{1,2},{2,3},{3,4},{4,5},{5,6},{6,7},{7,8},{8,9},{9,10},{10,1... | collective-permute-start | bytes 1304 | tf_op jit(solution)/shard_map/ppermute | solution.py:21
  23.7 4.3 %collective-permute-start.1 = (s32[2,2,3,128]{3,1,2,0:T(2,128)}, s32[2,2,3,128]{3,1,2,0:T(2,128)S(1)}, u32[]{:S(2)}, u32[]{:S(2)}) collective-permute-start(s32[2,2,3,128]{3,1,2,0:T(2,128)} %param.10), channel_id=1, source_target_pairs={{128,0},{256,128},{384,256},{129,1},{257,129},{385,257},{130,2},{2... | collective-permute-start | bytes 18440 | tf_op jit(solution)/shard_map/ppermute | solution.py:23
  28.0 6.8 %collective-permute-done.11 = s32[6,2,9]{2,1,0:T(2,128)S(1)} collective-permute-done((s32[6,2,9]{2,1,0:T(2,128)S(1)}, s32[6,2,9]{2,1,0:T(2,128)S(1)}, u32[]{:S(2)}, u32[]{:S(2)}) %collective-permute-start.11) | collective-permute-done | bytes 464 | tf_op jit(solution)/shard_map/ppermute | solution.py:23
  36.4 4.9 %collective-permute-start.13 = (bf16[2,2,128,256]{3,2,1,0:T(8,128)(2,1)}, bf16[2,2,128,256]{3,2,1,0:T(8,128)(2,1)S(1)}, u32[]{:S(2)}, u32[]{:S(2)}) collective-permute-start(bf16[2,2,128,256]{3,2,1,0:T(8,128)(2,1)} %param.8), channel_id=1, source_target_pairs={{128,0},{256,128},{384,256},{129,1},{257,129},{385,257},{130,2},{2... | collective-permute-start | bytes 786440 | tf_op jit(solution)/shard_map/ppermute | solution.py:23
  42.0 4.9 %collective-permute-start.6 = (bf16[6,2,128]{2,1,0:T(2,128)(2,1)S(1)}, bf16[6,2,128]{2,1,0:T(2,128)(2,1)S(1)}, u32[]{:S(2)}, u32[]{:S(2)}) collective-permute-start(bf16[6,2,128]{2,1,0:T(2,128)(2,1)S(1)} %constant_dynamic-update-slice_fusion), channel_id=1, source_target_pairs={{0,1},{1,2},{2,3},{3,4},{4,5},{5,6},{6,7},{7,8},{8,9},{9,10},{10,1... | collective-permute-start | bytes 9224 | tf_op jit(solution)/shard_map/ppermute | solution.py:21
  49.9 11.8 %collective-permute-start.14 = (bf16[6,2,128,256]{3,2,1,0:T(8,128)(2,1)S(1)}, bf16[6,2,128,256]{3,2,1,0:T(8,128)(2,1)S(1)}, u32[]{:S(2)}, u32[]{:S(2)}) collective-permute-start(bf16[6,2,128,256]{3,2,1,0:T(8,128)(2,1)S(1)} %constant_dynamic-update-slice_fusion.6), channel_id=1, source_target_pairs={{0,1},{1,2},{2,3},{3,4},{4,5},{5,6},{6,7},{7,8},{8,9},{9,10},{10,1... | collective-permute-start | bytes 2359304 | tf_op jit(solution)/shard_map/ppermute | solution.py:21
  64.3 11.8 %collective-permute-start.2 = (s32[6,2,3,128]{3,1,2,0:T(2,128)S(1)}, s32[6,2,3,128]{3,1,2,0:T(2,128)S(1)}, u32[]{:S(2)}, u32[]{:S(2)}) collective-permute-start(s32[6,2,3,128]{3,1,2,0:T(2,128)S(1)} %constant_dynamic-update-slice_fusion.9), channel_id=1, source_target_pairs={{0,1},{1,2},{2,3},{3,4},{4,5},{5,6},{6,7},{7,8},{8,9},{9,10},{10,1... | collective-permute-start | bytes 55304 | tf_op jit(solution)/shard_map/ppermute | solution.py:21
  79.1 12.6 %collective-permute-done.3 = s32[6,2,3,128]{3,1,2,0:T(2,128)S(1)} collective-permute-done((s32[6,2,3,128]{3,1,2,0:T(2,128)S(1)}, s32[6,2,3,128]{3,1,2,0:T(2,128)S(1)}, u32[]{:S(2)}, u32[]{:S(2)}) %collective-permute-start.3) | collective-permute-done | bytes 18464 | tf_op jit(solution)/shard_map/ppermute | solution.py:23
  94.3 75.8 %while.17 = (s32[]{:T(128)}, f32[128,256]{1,0:T(8,128)S(1)}, f32[14]{0:T(128)S(1)}, f32[4608]{0:T(1024)S(1)}, bf16[4608,256]{1,0:T(8,128)(2,1)S(1)}, /*index=5*/...) while((s32[]{:T(128)}, f32[128,256]{1,0:T(8,128)S(1)}, ...), condition=%wide.region_2.3_spmd.clone.clone, body=%wide.region_1.2_spmd.clone.clone.sunk | while | flops 416628480 | bytes 2989219 | solution.py:54
  95.6 2.3 %fusion.60 = f32[128,256]{1,0:T(8,128)S(1)} fusion(bf16[4608,256]{1,0:T(8,128)(2,1)S(1)} %get-tuple-element.416, s32[4608]{0:T(1024)S(1)} %get-tuple-element.420, s32[128]{0:T(128)S(1)} %get-tuple-element.421, s32[4608]{0:T(1024)S(1)} %get-tuple-element.418, s32[128]{0:T(128)S(1)} %get-tuple-element.419, s32[4608]{0:T(1024)S(1)} %get-tuple-element.422, ...), kind=kOutput, calls=%fused_computation.14.clone.1 | convolution fusion | flops 315555840 | bytes 2555908 | tf_op jit(solution)/shard_map/while/body/eval_jaxpr/dot_general | solution.py:43
  101.0 2.3 %fusion.60 = f32[128,256]{1,0:T(8,128)S(1)} fusion(bf16[4608,256]{1,0:T(8,128)(2,1)S(1)} %get-tuple-element.416, s32[4608]{0:T(1024)S(1)} %get-tuple-element.420, s32[128]{0:T(128)S(1)} %get-tuple-element.421, s32[4608]{0:T(1024)S(1)} %get-tuple-element.418, s32[128]{0:T(128)S(1)} %get-tuple-element.419, s32[4608]{0:T(1024)S(1)} %get-tuple-element.422, ...), kind=kOutput, calls=%fused_computation.14.clone.1 | convolution fusion | flops 315555840 | bytes 2555908 | tf_op jit(solution)/shard_map/while/body/eval_jaxpr/dot_general | solution.py:43
  106.4 2.3 %fusion.60 = f32[128,256]{1,0:T(8,128)S(1)} fusion(bf16[4608,256]{1,0:T(8,128)(2,1)S(1)} %get-tuple-element.416, s32[4608]{0:T(1024)S(1)} %get-tuple-element.420, s32[128]{0:T(128)S(1)} %get-tuple-element.421, s32[4608]{0:T(1024)S(1)} %get-tuple-element.418, s32[128]{0:T(128)S(1)} %get-tuple-element.419, s32[4608]{0:T(1024)S(1)} %get-tuple-element.422, ...), kind=kOutput, calls=%fused_computation.14.clone.1 | convolution fusion | flops 315555840 | bytes 2555908 | tf_op jit(solution)/shard_map/while/body/eval_jaxpr/dot_general | solution.py:43
  111.9 2.3 %fusion.60 = f32[128,256]{1,0:T(8,128)S(1)} fusion(bf16[4608,256]{1,0:T(8,128)(2,1)S(1)} %get-tuple-element.416, s32[4608]{0:T(1024)S(1)} %get-tuple-element.420, s32[128]{0:T(128)S(1)} %get-tuple-element.421, s32[4608]{0:T(1024)S(1)} %get-tuple-element.418, s32[128]{0:T(128)S(1)} %get-tuple-element.419, s32[4608]{0:T(1024)S(1)} %get-tuple-element.422, ...), kind=kOutput, calls=%fused_computation.14.clone.1 | convolution fusion | flops 315555840 | bytes 2555908 | tf_op jit(solution)/shard_map/while/body/eval_jaxpr/dot_general | solution.py:43
  117.3 2.3 %fusion.60 = f32[128,256]{1,0:T(8,128)S(1)} fusion(bf16[4608,256]{1,0:T(8,128)(2,1)S(1)} %get-tuple-element.416, s32[4608]{0:T(1024)S(1)} %get-tuple-element.420, s32[128]{0:T(128)S(1)} %get-tuple-element.421, s32[4608]{0:T(1024)S(1)} %get-tuple-element.418, s32[128]{0:T(128)S(1)} %get-tuple-element.419, s32[4608]{0:T(1024)S(1)} %get-tuple-element.422, ...), kind=kOutput, calls=%fused_computation.14.clone.1 | convolution fusion | flops 315555840 | bytes 2555908 | tf_op jit(solution)/shard_map/while/body/eval_jaxpr/dot_general | solution.py:43
  122.7 2.3 %fusion.60 = f32[128,256]{1,0:T(8,128)S(1)} fusion(bf16[4608,256]{1,0:T(8,128)(2,1)S(1)} %get-tuple-element.416, s32[4608]{0:T(1024)S(1)} %get-tuple-element.420, s32[128]{0:T(128)S(1)} %get-tuple-element.421, s32[4608]{0:T(1024)S(1)} %get-tuple-element.418, s32[128]{0:T(128)S(1)} %get-tuple-element.419, s32[4608]{0:T(1024)S(1)} %get-tuple-element.422, ...), kind=kOutput, calls=%fused_computation.14.clone.1 | convolution fusion | flops 315555840 | bytes 2555908 | tf_op jit(solution)/shard_map/while/body/eval_jaxpr/dot_general | solution.py:43
  128.1 2.3 %fusion.60 = f32[128,256]{1,0:T(8,128)S(1)} fusion(bf16[4608,256]{1,0:T(8,128)(2,1)S(1)} %get-tuple-element.416, s32[4608]{0:T(1024)S(1)} %get-tuple-element.420, s32[128]{0:T(128)S(1)} %get-tuple-element.421, s32[4608]{0:T(1024)S(1)} %get-tuple-element.418, s32[128]{0:T(128)S(1)} %get-tuple-element.419, s32[4608]{0:T(1024)S(1)} %get-tuple-element.422, ...), kind=kOutput, calls=%fused_computation.14.clone.1 | convolution fusion | flops 315555840 | bytes 2555908 | tf_op jit(solution)/shard_map/while/body/eval_jaxpr/dot_general | solution.py:43
  133.5 2.3 %fusion.60 = f32[128,256]{1,0:T(8,128)S(1)} fusion(bf16[4608,256]{1,0:T(8,128)(2,1)S(1)} %get-tuple-element.416, s32[4608]{0:T(1024)S(1)} %get-tuple-element.420, s32[128]{0:T(128)S(1)} %get-tuple-element.421, s32[4608]{0:T(1024)S(1)} %get-tuple-element.418, s32[128]{0:T(128)S(1)} %get-tuple-element.419, s32[4608]{0:T(1024)S(1)} %get-tuple-element.422, ...), kind=kOutput, calls=%fused_computation.14.clone.1 | convolution fusion | flops 315555840 | bytes 2555908 | tf_op jit(solution)/shard_map/while/body/eval_jaxpr/dot_general | solution.py:43
  139.0 2.3 %fusion.60 = f32[128,256]{1,0:T(8,128)S(1)} fusion(bf16[4608,256]{1,0:T(8,128)(2,1)S(1)} %get-tuple-element.416, s32[4608]{0:T(1024)S(1)} %get-tuple-element.420, s32[128]{0:T(128)S(1)} %get-tuple-element.421, s32[4608]{0:T(1024)S(1)} %get-tuple-element.418, s32[128]{0:T(128)S(1)} %get-tuple-element.419, s32[4608]{0:T(1024)S(1)} %get-tuple-element.422, ...), kind=kOutput, calls=%fused_computation.14.clone.1 | convolution fusion | flops 315555840 | bytes 2555908 | tf_op jit(solution)/shard_map/while/body/eval_jaxpr/dot_general | solution.py:43
  144.4 2.3 %fusion.60 = f32[128,256]{1,0:T(8,128)S(1)} fusion(bf16[4608,256]{1,0:T(8,128)(2,1)S(1)} %get-tuple-element.416, s32[4608]{0:T(1024)S(1)} %get-tuple-element.420, s32[128]{0:T(128)S(1)} %get-tuple-element.421, s32[4608]{0:T(1024)S(1)} %get-tuple-element.418, s32[128]{0:T(128)S(1)} %get-tuple-element.419, s32[4608]{0:T(1024)S(1)} %get-tuple-element.422, ...), kind=kOutput, calls=%fused_computation.14.clone.1 | convolution fusion | flops 315555840 | bytes 2555908 | tf_op jit(solution)/shard_map/while/body/eval_jaxpr/dot_general | solution.py:43
  149.8 2.3 %fusion.60 = f32[128,256]{1,0:T(8,128)S(1)} fusion(bf16[4608,256]{1,0:T(8,128)(2,1)S(1)} %get-tuple-element.416, s32[4608]{0:T(1024)S(1)} %get-tuple-element.420, s32[128]{0:T(128)S(1)} %get-tuple-element.421, s32[4608]{0:T(1024)S(1)} %get-tuple-element.418, s32[128]{0:T(128)S(1)} %get-tuple-element.419, s32[4608]{0:T(1024)S(1)} %get-tuple-element.422, ...), kind=kOutput, calls=%fused_computation.14.clone.1 | convolution fusion | flops 315555840 | bytes 2555908 | tf_op jit(solution)/shard_map/while/body/eval_jaxpr/dot_general | solution.py:43
  155.2 2.3 %fusion.60 = f32[128,256]{1,0:T(8,128)S(1)} fusion(bf16[4608,256]{1,0:T(8,128)(2,1)S(1)} %get-tuple-element.416, s32[4608]{0:T(1024)S(1)} %get-tuple-element.420, s32[128]{0:T(128)S(1)} %get-tuple-element.421, s32[4608]{0:T(1024)S(1)} %get-tuple-element.418, s32[128]{0:T(128)S(1)} %get-tuple-element.419, s32[4608]{0:T(1024)S(1)} %get-tuple-element.422, ...), kind=kOutput, calls=%fused_computation.14.clone.1 | convolution fusion | flops 315555840 | bytes 2555908 | tf_op jit(solution)/shard_map/while/body/eval_jaxpr/dot_general | solution.py:43
  160.6 2.3 %fusion.60 = f32[128,256]{1,0:T(8,128)S(1)} fusion(bf16[4608,256]{1,0:T(8,128)(2,1)S(1)} %get-tuple-element.416, s32[4608]{0:T(1024)S(1)} %get-tuple-element.420, s32[128]{0:T(128)S(1)} %get-tuple-element.421, s32[4608]{0:T(1024)S(1)} %get-tuple-element.418, s32[128]{0:T(128)S(1)} %get-tuple-element.419, s32[4608]{0:T(1024)S(1)} %get-tuple-element.422, ...), kind=kOutput, calls=%fused_computation.14.clone.1 | convolution fusion | flops 315555840 | bytes 2555908 | tf_op jit(solution)/shard_map/while/body/eval_jaxpr/dot_general | solution.py:43
  (125 shorter events, 65.9 us)
Async XLA Ops:
  0.0 12.0 %collective-permute-start.8 = (s32[2,2,9]{2,1,0:T(2,128)}, s32[2,2,9]{2,1,0:T(2,128)S(1)}, u32[]{:S(2)}, u32[]{:S(2)}) collective-permute-start(s32[2,2,9]{2,1,0:T(2,128)} %param.9), channel_id=1, source_target_pairs={{0,128},{128,256},{256,384},{1,129},{129,257},{257,385},{2,130},{1... | collective-permute-start | bytes 440 | tf_op jit(solution)/shard_map/ppermute | solution.py:21
  1.3 11.4 %collective-permute-start.9 = (s32[2,2,9]{2,1,0:T(2,128)}, s32[2,2,9]{2,1,0:T(2,128)S(1)}, u32[]{:S(2)}, u32[]{:S(2)}) collective-permute-start(s32[2,2,9]{2,1,0:T(2,128)} %param.9), channel_id=1, source_target_pairs={{128,0},{256,128},{384,256},{129,1},{257,129},{385,257},{130,2},{2... | collective-permute-start | bytes 440 | tf_op jit(solution)/shard_map/ppermute | solution.py:23
  5.3 31.1 %collective-permute-start.4 = (bf16[2,2,128]{2,1,0:T(2,128)(2,1)}, bf16[2,2,128]{2,1,0:T(2,128)(2,1)S(1)}, u32[]{:S(2)}, u32[]{:S(2)}) collective-permute-start(bf16[2,2,128]{2,1,0:T(2,128)(2,1)} %param.11), channel_id=1, source_target_pairs={{0,128},{128,256},{256,384},{1,129},{129,257},{257,385},{2,130},{1... | collective-permute-start | bytes 3080 | tf_op jit(solution)/shard_map/ppermute | solution.py:21
  6.6 35.4 %collective-permute-start.5 = (bf16[2,2,128]{2,1,0:T(2,128)(2,1)}, bf16[2,2,128]{2,1,0:T(2,128)(2,1)S(1)}, u32[]{:S(2)}, u32[]{:S(2)}) collective-permute-start(bf16[2,2,128]{2,1,0:T(2,128)(2,1)} %param.11), channel_id=1, source_target_pairs={{128,0},{256,128},{384,256},{129,1},{257,129},{385,257},{130,2},{2... | collective-permute-start | bytes 3080 | tf_op jit(solution)/shard_map/ppermute | solution.py:23
  10.6 36.3 %collective-permute-start = (s32[2,2,3,128]{3,1,2,0:T(2,128)}, s32[2,2,3,128]{3,1,2,0:T(2,128)S(1)}, u32[]{:S(2)}, u32[]{:S(2)}) collective-permute-start(s32[2,2,3,128]{3,1,2,0:T(2,128)} %param.10), channel_id=1, source_target_pairs={{0,128},{128,256},{256,384},{1,129},{129,257},{257,385},{2,130},{1... | collective-permute-start | bytes 18440 | tf_op jit(solution)/shard_map/ppermute | solution.py:21
  12.7 11.0 %collective-permute-start.10 = (s32[6,2,9]{2,1,0:T(2,128)S(1)}, s32[6,2,9]{2,1,0:T(2,128)S(1)}, u32[]{:S(2)}, u32[]{:S(2)}) collective-permute-start(s32[6,2,9]{2,1,0:T(2,128)S(1)} %constant_dynamic-update-slice_fusion.3), channel_id=1, source_target_pairs={{0,1},{1,2},{2,3},{3,4},{4,5},{5,6},{6,7},{7,8},{8,9},{9,10},{10,1... | collective-permute-start | bytes 1304 | tf_op jit(solution)/shard_map/ppermute | solution.py:21
  21.7 13.1 %collective-permute-start.11 = (s32[6,2,9]{2,1,0:T(2,128)S(1)}, s32[6,2,9]{2,1,0:T(2,128)S(1)}, u32[]{:S(2)}, u32[]{:S(2)}) collective-permute-start(s32[6,2,9]{2,1,0:T(2,128)S(1)} %constant_dynamic-update-slice_fusion.3), channel_id=1, source_target_pairs={{1,0},{2,1},{3,2},{4,3},{5,4},{6,5},{7,6},{8,7},{9,8},{10,9},{11,1... | collective-permute-start | bytes 1304 | tf_op jit(solution)/shard_map/ppermute | solution.py:23
  23.7 40.6 %collective-permute-start.1 = (s32[2,2,3,128]{3,1,2,0:T(2,128)}, s32[2,2,3,128]{3,1,2,0:T(2,128)S(1)}, u32[]{:S(2)}, u32[]{:S(2)}) collective-permute-start(s32[2,2,3,128]{3,1,2,0:T(2,128)} %param.10), channel_id=1, source_target_pairs={{128,0},{256,128},{384,256},{129,1},{257,129},{385,257},{130,2},{2... | collective-permute-start | bytes 18440 | tf_op jit(solution)/shard_map/ppermute | solution.py:23
  34.8 14.0 %collective-permute-start.12 = (bf16[2,2,128,256]{3,2,1,0:T(8,128)(2,1)}, bf16[2,2,128,256]{3,2,1,0:T(8,128)(2,1)S(1)}, u32[]{:S(2)}, u32[]{:S(2)}) collective-permute-start(bf16[2,2,128,256]{3,2,1,0:T(8,128)(2,1)} %param.8), channel_id=1, source_target_pairs={{0,128},{128,256},{256,384},{1,129},{129,257},{257,385},{2,130},{1... | collective-permute-start | bytes 786440 | tf_op jit(solution)/shard_map/ppermute | solution.py:21
  36.4 13.5 %collective-permute-start.13 = (bf16[2,2,128,256]{3,2,1,0:T(8,128)(2,1)}, bf16[2,2,128,256]{3,2,1,0:T(8,128)(2,1)S(1)}, u32[]{:S(2)}, u32[]{:S(2)}) collective-permute-start(bf16[2,2,128,256]{3,2,1,0:T(8,128)(2,1)} %param.8), channel_id=1, source_target_pairs={{128,0},{256,128},{384,256},{129,1},{257,129},{385,257},{130,2},{2... | collective-permute-start | bytes 786440 | tf_op jit(solution)/shard_map/ppermute | solution.py:23
  42.0 34.1 %collective-permute-start.6 = (bf16[6,2,128]{2,1,0:T(2,128)(2,1)S(1)}, bf16[6,2,128]{2,1,0:T(2,128)(2,1)S(1)}, u32[]{:S(2)}, u32[]{:S(2)}) collective-permute-start(bf16[6,2,128]{2,1,0:T(2,128)(2,1)S(1)} %constant_dynamic-update-slice_fusion), channel_id=1, source_target_pairs={{0,1},{1,2},{2,3},{3,4},{4,5},{5,6},{6,7},{7,8},{8,9},{9,10},{10,1... | collective-permute-start | bytes 9224 | tf_op jit(solution)/shard_map/ppermute | solution.py:21
  46.9 31.1 %collective-permute-start.7 = (bf16[6,2,128]{2,1,0:T(2,128)(2,1)S(1)}, bf16[6,2,128]{2,1,0:T(2,128)(2,1)S(1)}, u32[]{:S(2)}, u32[]{:S(2)}) collective-permute-start(bf16[6,2,128]{2,1,0:T(2,128)(2,1)S(1)} %constant_dynamic-update-slice_fusion), channel_id=1, source_target_pairs={{1,0},{2,1},{3,2},{4,3},{5,4},{6,5},{7,6},{8,7},{9,8},{10,9},{11,1... | collective-permute-start | bytes 9224 | tf_op jit(solution)/shard_map/ppermute | solution.py:23
  49.9 41.9 %collective-permute-start.14 = (bf16[6,2,128,256]{3,2,1,0:T(8,128)(2,1)S(1)}, bf16[6,2,128,256]{3,2,1,0:T(8,128)(2,1)S(1)}, u32[]{:S(2)}, u32[]{:S(2)}) collective-permute-start(bf16[6,2,128,256]{3,2,1,0:T(8,128)(2,1)S(1)} %constant_dynamic-update-slice_fusion.6), channel_id=1, source_target_pairs={{0,1},{1,2},{2,3},{3,4},{4,5},{5,6},{6,7},{7,8},{8,9},{9,10},{10,1... | collective-permute-start | bytes 2359304 | tf_op jit(solution)/shard_map/ppermute | solution.py:21
  61.7 31.0 %collective-permute-start.15 = (bf16[6,2,128,256]{3,2,1,0:T(8,128)(2,1)S(1)}, bf16[6,2,128,256]{3,2,1,0:T(8,128)(2,1)}, u32[]{:S(2)}, u32[]{:S(2)}) collective-permute-start(bf16[6,2,128,256]{3,2,1,0:T(8,128)(2,1)S(1)} %constant_dynamic-update-slice_fusion.6), channel_id=1, source_target_pairs={{1,0},{2,1},{3,2},{4,3},{5,4},{6,5},{7,6},{8,7},{9,8},{10,9},{11,1... | collective-permute-start | bytes 2359304 | tf_op jit(solution)/shard_map/ppermute | solution.py:23
  64.3 14.8 %collective-permute-start.2 = (s32[6,2,3,128]{3,1,2,0:T(2,128)S(1)}, s32[6,2,3,128]{3,1,2,0:T(2,128)S(1)}, u32[]{:S(2)}, u32[]{:S(2)}) collective-permute-start(s32[6,2,3,128]{3,1,2,0:T(2,128)S(1)} %constant_dynamic-update-slice_fusion.9), channel_id=1, source_target_pairs={{0,1},{1,2},{2,3},{3,4},{4,5},{5,6},{6,7},{7,8},{8,9},{9,10},{10,1... | collective-permute-start | bytes 55304 | tf_op jit(solution)/shard_map/ppermute | solution.py:21
  76.1 15.6 %collective-permute-start.3 = (s32[6,2,3,128]{3,1,2,0:T(2,128)S(1)}, s32[6,2,3,128]{3,1,2,0:T(2,128)S(1)}, u32[]{:S(2)}, u32[]{:S(2)}) collective-permute-start(s32[6,2,3,128]{3,1,2,0:T(2,128)S(1)} %constant_dynamic-update-slice_fusion.9), channel_id=1, source_target_pairs={{1,0},{2,1},{3,2},{4,3},{5,4},{6,5},{7,6},{8,7},{9,8},{10,9},{11,1... | collective-permute-start | bytes 55304 | tf_op jit(solution)/shard_map/ppermute | solution.py:23
  91.8 2.6 %copy-start.1 = (f32[14]{0:T(128)S(1)}, f32[14]{0:T(128)}, u32[]{:S(2)}) copy-start(f32[14]{0:T(128)} %param.12) | copy-start | bytes 172
  91.8 0.9 copy-start
  170.2 0.7 copy-start.2
where the time goes:
time: 173 us; the launch traced here: 171 us
  starting transfers between devices  67.4 us (39%)
  matrix products  37.4 us (22%)
  other arithmetic  31.2 us (18%)
  waiting for transfers between devices  20.4 us (12%)
  local copies, waits for them, and re-layouts  13.4 us (8%)
    ppermute x8, starting transfers between devices, padded(): lax.ppermute(tail, axis, [(i, (i + 1) % count) for i in range(ends)])  42.6 us
    dot_general x14, matrix products, add_class(): stacked = jnp.dot(amplitude, samples_in, preferred_element_type=jnp.float32)  32.2 us
    ppermute x8, starting transfers between devices, padded(): lax.ppermute(head, axis, [((i + 1) % count, i) for i in range(ends)])  24.9 us
    ppermute x8, waiting for transfers between devices, padded(): lax.ppermute(head, axis, [((i + 1) % count, i) for i in range(ends)])  19.4 us
    sub x14, other arithmetic, add_class(): 1.0 - fraction[None, :]  10.3 us
    add x14, other arithmetic, add_class(): first_sample[None, :] + 1  10 us
    convert_element_type x14, other arithmetic, add_class(): scaled = (live_weights * class_weight[level]).astype(jnp.bfloat16)  8.83 us
    dynamic_slice x14, local copies, waits for them, and re-layouts, add_class(): scaled = (live_weights * class_weight[level]).astype(jnp.bfloat16)  8.68 us
  transfers between devices with their start and end apart: 16, of which 3 were waited for; matrix products, arithmetic and copies ran while one was open for 2% of the time, Pallas kernels for 0%

commit v1 on v0

v1 whole, which is shorter than its diff:
```python
import jax
import jax.numpy as jnp
from jax import lax
from jax.experimental import pallas as pl
from jax.experimental.pallas import tpu as pltpu
from jax.sharding import PartitionSpec as P

NS = 256
NT = 256
TR = 128
NB = 4
NJ = NB * TR
NC = 14
NOC = 8
PX = 16
PY = 8
PTS = PX * PY
L_OWN, L_X, L_Y, L_XY = 3, 5, 4, 6
LV = 7
MESH = pl.DeviceIdType.MESH
BF = jnp.bfloat16
F32 = jnp.float32


def kernel(
    tr_ref, ap_ref, geo_ref, wt_ref, cw_ref, tt_ref, out_ref,
    t_ref, v_ref, a_ref, fo, fx, acc, so, sp, sx, sf, ro, rp, rx, rf, send, recv,
):
    gx = lax.axis_index("gx")
    gy = lax.axis_index("gy")
    ngx = lax.axis_size("gx")
    ngy = lax.axis_size("gy")
    core = lax.rem(gy, 2)
    step = 2 * core - 1
    partner = gy - step
    far = gy + step
    has_lo = gx > 0
    has_hi = gx < ngx - 1
    has_far = jnp.logical_and(far >= 0, far < ngy)

    barrier = pltpu.get_barrier_semaphore()

    def greet(dev):
        pl.semaphore_signal(barrier, inc=1, device_id=dev, device_id_type=MESH)

    pl.when(has_far)(lambda: greet((gx, far)))
    pl.when(has_lo)(lambda: greet((gx - 1, gy)))
    pl.when(has_hi)(lambda: greet((gx + 1, gy)))
    greet((gx, partner))

    def copy(src, dst, k, dev):
        return pltpu.make_async_remote_copy(
            src_ref=src, dst_ref=dst, send_sem=send.at[k], recv_sem=recv.at[k], device_id=dev, device_id_type=MESH
        )

    lo, hi, pa, fa = (gx - 1, gy), (gx + 1, gy), (gx, partner), (gx, far)
    to_hi_o = copy(so.at[1], ro.at[0], 0, hi)
    to_lo_o = copy(so.at[0], ro.at[1], 1, lo)
    to_pa = copy(sp, rp, 2, pa)
    to_hi_x = copy(sx.at[1], rx.at[0], 3, hi)
    to_lo_x = copy(sx.at[0], rx.at[1], 4, lo)
    to_fa = copy(sf, rf, 5, fa)

    traces = tr_ref[...]
    sample = lax.broadcasted_iota(jnp.int32, (NS, NT), 0).astype(F32).astype(BF)
    zero = jnp.zeros((NS, NT), BF)
    for c in range(NC):
        q = tt_ref[c : c + 1, :]
        first = q // 4
        frac = (q % 4).astype(F32) * 0.25
        s0 = jnp.broadcast_to(first.astype(F32), (NS, NT)).astype(BF)
        s1 = jnp.broadcast_to((first + 1).astype(F32), (NS, NT)).astype(BF)
        w1 = jnp.broadcast_to(frac, (NS, NT)).astype(BF)
        w0 = jnp.broadcast_to(1.0 - frac, (NS, NT)).astype(BF)
        interp = jnp.where(sample == s0, w0, jnp.where(sample == s1, w1, zero))
        t_ref[c] = jnp.dot(traces, interp, preferred_element_type=F32).astype(BF)

    for b in range(NB):
        i, k = b // 2, b % 2
        oc_row = jnp.broadcast_to(geo_ref[i, k, 2:3, :], (TR, TR)).astype(F32)
        oc = jnp.transpose(oc_row)
        oc = jnp.concatenate([oc, oc], axis=1).astype(BF)
        for r in range(0, TR, 16):
            o = oc[r : r + 16]
            row = b * TR + r
            b2 = o >= 4
            o = jnp.where(b2, o - 4, o)
            b1 = o >= 2
            o = jnp.where(b1, o - 2, o)
            b0 = o >= 1
            t = [t_ref[c, row : row + 16, :] for c in range(NC)]
            t = [jnp.where(b2, t[c + 4], t[c]) for c in range(NC - 4)]
            t = [jnp.where(b1, t[c + 2], t[c]) for c in range(NC - 6)]
            t = [jnp.where(b0, t[c + 1], t[c]) for c in range(NC - 7)]
            for d in range(LV):
                v_ref[d * NJ + row : d * NJ + row + 16, :] = t[d]

    row16 = lax.broadcasted_iota(jnp.int32, (16, TR), 0)
    upper = (row16 // 8).astype(F32) * 0.125
    py = (row16 % 8).astype(F32) * 0.125
    ex, ey, wd = [], [], []
    for b in range(NB):
        i, k = b // 2, b % 2
        mx = (geo_ref[i, k, 0:1, :] - gx * PX).astype(F32) * 0.125
        my = (geo_ref[i, k, 1:2, :] - gy * PY).astype(F32) * 0.125
        ex.append((upper - mx).astype(BF))
        ey.append((py - my).astype(BF))
        oc = geo_ref[i, k, 2:3, :]
        w = wt_ref[i, k : k + 1, :].astype(F32)
        levels = []
        for d in range(LV):
            cw = jnp.zeros((1, TR), F32)
            for o in range(NOC):
                if o + d < NC:
                    cw = jnp.where(oc == o, cw_ref[o + d], cw)
            levels.append(jnp.broadcast_to(w * cw, (16, TR)).astype(BF))
        wd.append(levels)
    zero16 = jnp.zeros((16, TR), BF)

    def live_of(b, dx, kind):
        i, k = b // 2, b % 2
        base = (dx + 1) * 3
        mid = ap_ref[i, k, base + 1]
        up = ap_ref[i, k, base + 2]
        down = ap_ref[i, k, base]
        if kind == 0:
            return mid
        if kind == 1:
            return jnp.where(core == 1, up, down)
        return jnp.where(core == 1, down, up)

    def tile(slot, dx, kind, nlev):
        shift = {0: 0, 1: step, 2: -step}[kind]
        for b in range(NB):
            gone = (1 - live_of(b, dx, kind)).astype(F32) * 64.0
            dy = jnp.abs(ey[b] + shift.astype(F32).astype(BF) if kind else ey[b]) + gone.astype(BF)
            for g in range(PX // 2):
                dist = jnp.abs(ex[b] + jnp.asarray(2 * dx + 0.25 * g, BF)) + dy
                level = jnp.floor(dist)
                for d in range(nlev):
                    a_ref[slot, 16 * g : 16 * g + 16, d * NJ + b * TR : d * NJ + b * TR + TR] = jnp.where(
                        level == d, wd[b][d], zero16
                    )

    def migrate(slot, count, nlev):
        lhs = a_ref[slot : slot + count, :, : nlev * NJ].reshape(count * PTS, nlev * NJ)
        return jnp.dot(lhs, v_ref[: nlev * NJ, :], preferred_element_type=F32)

    tile(0, -1, 1, LV)
    tile(1, 1, 1, LV)
    so[...] = migrate(0, 2, LV).astype(BF).reshape(2, PTS, NT)
    count = has_lo.astype(jnp.int32) + has_hi.astype(jnp.int32) + has_far.astype(jnp.int32) + 1
    pl.semaphore_wait(barrier, count)
    pl.when(has_hi)(lambda: to_hi_o.start())
    pl.when(has_lo)(lambda: to_lo_o.start())
    tile(2, 0, 1, L_Y)
    fo[...] = migrate(2, 1, L_Y)
    tile(3, -1, 2, LV)
    tile(4, 1, 2, LV)
    corners = migrate(3, 2, LV).astype(BF)
    sp[0] = corners[:PTS]
    sp[1] = corners[PTS:]
    tile(5, 0, 2, L_Y)
    sp[2] = migrate(5, 1, L_Y).astype(BF)
    to_pa.start()

    @pl.when(has_lo)
    def _():
        to_hi_o.wait_recv()
        fo[...] += ro[0].astype(F32)

    @pl.when(has_hi)
    def _():
        to_lo_o.wait_recv()
        fo[...] += ro[1].astype(F32)

    @pl.when(has_far)
    def _():
        sf[...] = fo[...].astype(BF)
        to_fa.start()

    tile(6, -1, 0, L_X)
    tile(7, 1, 0, L_X)
    fx[...] = migrate(6, 2, L_X)
    to_pa.wait_recv()
    sx[0] = (fx[:PTS] + rp[0].astype(F32)).astype(BF)
    sx[1] = (fx[PTS:] + rp[1].astype(F32)).astype(BF)
    pl.when(has_hi)(lambda: to_hi_x.start())
    pl.when(has_lo)(lambda: to_lo_x.start())
    tile(8, 0, 0, L_OWN)
    acc[...] = migrate(8, 1, L_OWN) + rp[2].astype(F32)

    @pl.when(has_lo)
    def _():
        to_hi_x.wait_recv()
        acc[...] += rx[0].astype(F32)

    @pl.when(has_hi)
    def _():
        to_lo_x.wait_recv()
        acc[...] += rx[1].astype(F32)

    @pl.when(has_far)
    def _():
        to_fa.wait_recv()
        acc[...] += rf[...].astype(F32)

    out_ref[...] = acc[...].reshape(PX, PY, NT)

    to_pa.wait_send()
    pl.when(has_far)(lambda: to_fa.wait_send())

    @pl.when(has_hi)
    def _():
        to_hi_o.wait_send()
        to_hi_x.wait_send()

    @pl.when(has_lo)
    def _():
        to_lo_o.wait_send()
        to_lo_x.wait_send()


def per_device(traces, aperture, geometry, trace_weight, class_weight, traveltime):
    vmem = pl.BlockSpec(memory_space=pltpu.VMEM)
    smem = pl.BlockSpec(memory_space=pltpu.SMEM)
    tile = (PTS, NT)
    return pl.pallas_call(
        kernel,
        out_shape=jax.ShapeDtypeStruct((PX, PY, NT), F32),
        in_specs=[vmem, smem, vmem, vmem, smem, vmem],
        out_specs=vmem,
        scratch_shapes=[
            pltpu.VMEM((NC, NJ, NT), BF),
            pltpu.VMEM((LV * NJ, NT), BF),
            pltpu.VMEM((9, PTS, LV * NJ), BF),
            pltpu.VMEM(tile, F32),
            pltpu.VMEM((2 * PTS, NT), F32),
            pltpu.VMEM(tile, F32),
            pltpu.VMEM((2,) + tile, BF),
            pltpu.VMEM((3,) + tile, BF),
            pltpu.VMEM((2,) + tile, BF),
            pltpu.VMEM(tile, BF),
            pltpu.VMEM((2,) + tile, BF),
            pltpu.VMEM((3,) + tile, BF),
            pltpu.VMEM((2,) + tile, BF),
            pltpu.VMEM(tile, BF),
            pltpu.SemaphoreType.DMA((6,)),
            pltpu.SemaphoreType.DMA((6,)),
        ],
        compiler_params=pltpu.CompilerParams(
            collective_id=0, has_side_effects=True, vmem_limit_bytes=60 * 1024 * 1024
        ),
        cost_estimate=pl.CostEstimate(flops=3_000_000_000, bytes_accessed=2_000_000, transcendentals=0),
        name="migrate",
    )(traces.reshape(NJ, NS), aperture, geometry, trace_weight, class_weight, traveltime)


def solution(mesh):
    return jax.shard_map(
        per_device,
        mesh=mesh,
        in_specs=(
            P("gx", "gy", None, None),
            P("gx", "gy", None),
            P("gx", "gy", None, None),
            P("gx", "gy", None),
            P(),
            P(),
        ),
        out_specs=P("gx", "gy", None),
        check_vma=False,
    )
```

time: 173 us -> 21.7 us (0.13)
  the two profiles are of different devices: /device:TPU:255 before, /device:TPU:239 now
where the time goes in v1:
time: 21.7 us; the launch traced here: 21.5 us
  Pallas kernels  18.6 us (86%)
  local copies, waits for them, and re-layouts  2.86 us (13%)
    pallas_call x1, Pallas kernels, per_device(): pl.pallas_call(kernel, out_shape=jax.ShapeDtypeStruct((PX, PY, NT), F32),...  18.6 us
    unnamed x2, local copies, waits for them, and re-layouts  2.86 us

profile of v1, /device:TPU:239, one launch (start us, length us, event | category | flops | bytes accessed | tf_op | source)
XLA Modules:
  0.0 21.5 jit_solution(9646747099268687059)
XLA Ops:
  0.0 1.3 %copy.7.geo_ref = s32[2,2,3,128]{3,2,1,0:T(4,128)} copy(s32[2,2,3,128]{3,1,2,0:T(2,128)} %param.8) | data formatting | bytes 12288 | tf_op args[2]
  1.3 18.6 %migrate.1 = f32[16,8,256]{2,1,0:T(8,128)} custom-call(bf16[512,256]{1,0:T(8,128)(2,1)} %bitcast.1, s32[2,2,9]{2,1,0:T(2,128)} %ap_ref.1, s32[2,2,3,128]{3,2,1,0:T(4,128)} %copy.7.geo_ref, bf16[2,2,128]{2,1,0:T(2,128)(2,1)} %wt_ref.1, f32[14]{0:T(128)} %cw_ref.1, s32[14,256]{1,0:T(8,128)} %tt_ref.1), custom_call_target="tpu_custom_call" | custom-call | flops 3000000000 | bytes 2000000 | tf_op jit(solution)/shard_map/migrate/pallas_call | solution.py:228
  19.9 1.6 %copy.9 = f32[16,8,256]{2,1,0:T(8,128)} copy(f32[16,8,256]{2,1,0:T(8,128)} %migrate.1) | data formatting | bytes 262144

commit v2 on v0

v2 whole, which is shorter than its diff:
```python
import jax
import jax.numpy as jnp
from jax import lax
from jax.experimental import pallas as pl
from jax.experimental.pallas import tpu as pltpu
from jax.sharding import PartitionSpec as P

NS = 256
NT = 256
TR = 128
NB = 4
NJ = NB * TR
NC = 14
NOC = 8
PX = 16
PY = 8
PTS = PX * PY
L_OWN, L_X, L_Y, L_XY = 3, 5, 4, 6
LV = 7
MESH = pl.DeviceIdType.MESH
BF = jnp.bfloat16
F32 = jnp.float32


def kernel(
    tr_hbm, ap_hbm, geo_hbm, wt_hbm, cw_hbm, tt_hbm, out_ref,
    tr_ref, ap_ref, geo_ref, wt_ref, cw_ref, tt_ref, i_ref, t_ref, v_ref, a_ref, sent, got, load, send, recv,
):
    gx = lax.axis_index("gx")
    gy = lax.axis_index("gy")
    ngx = lax.axis_size("gx")
    ngy = lax.axis_size("gy")
    core = lax.rem(gy, 2)
    step = 2 * core - 1
    has_x = {-1: gx > 0, 1: gx < ngx - 1, 0: None}
    has_far = jnp.logical_and(gy + step >= 0, gy + step < ngy)

    order = [(0, 1), (-1, 1), (1, 1), (-1, 2), (1, 2), (-1, 0), (1, 0), (0, 2)]

    def device(dx, kind):
        return (gx + dx, gy + {0: 0, 1: step, 2: -step}[kind])

    def exists(dx, kind):
        side = has_x[dx]
        if kind == 1:
            return has_far if side is None else jnp.logical_and(side, has_far)
        return side

    def guarded(cond, body):
        if cond is None:
            body()
        else:
            pl.when(cond)(body)

    barrier = pltpu.get_barrier_semaphore()
    count = jnp.int32(0)
    for n in order:
        cond = exists(*n)
        guarded(
            cond,
            lambda n=n: pl.semaphore_signal(barrier, inc=1, device_id=device(*n), device_id_type=MESH),
        )
        count = count + (1 if cond is None else cond.astype(jnp.int32))

    loads = [
        pltpu.make_async_copy(src, dst, load.at[k])
        for k, (src, dst) in enumerate(
            [(tt_hbm, tt_ref), (geo_hbm, geo_ref), (wt_hbm, wt_ref), (cw_hbm, cw_ref), (ap_hbm, ap_ref), (tr_hbm, tr_ref)]
        )
    ]
    for copy in loads:
        copy.start()

    copies = []
    for k, (dx, kind) in enumerate(order):
        copies.append(
            pltpu.make_async_remote_copy(
                src_ref=sent.at[k],
                dst_ref=got.at[k],
                send_sem=send.at[k],
                recv_sem=recv.at[k],
                device_id=device(dx, kind),
                device_id_type=MESH,
            )
        )

    loads[0].wait()
    sample = lax.broadcasted_iota(jnp.int32, (NS, NT), 0).astype(F32).astype(BF)
    zero = jnp.zeros((NS, NT), BF)
    for c in range(NC):
        q = tt_ref[c : c + 1, :]
        first = q // 4
        frac = (q % 4).astype(F32) * 0.25
        s0 = jnp.broadcast_to(first.astype(F32), (NS, NT)).astype(BF)
        s1 = jnp.broadcast_to((first + 1).astype(F32), (NS, NT)).astype(BF)
        w1 = jnp.broadcast_to(frac, (NS, NT)).astype(BF)
        w0 = jnp.broadcast_to(1.0 - frac, (NS, NT)).astype(BF)
        i_ref[c] = jnp.where(sample == s0, w0, jnp.where(sample == s1, w1, zero))

    for copy in loads[1:5]:
        copy.wait()
    row16 = lax.broadcasted_iota(jnp.int32, (16, TR), 0)
    upper = (row16 // 8).astype(F32) * 0.125
    py = (row16 % 8).astype(F32) * 0.125
    ex, ey, wd = [], [], []
    for b in range(NB):
        i, k = b // 2, b % 2
        mx = (geo_ref[i, 0, k : k + 1, :] - gx * PX).astype(F32) * 0.125
        my = (geo_ref[i, 1, k : k + 1, :] - gy * PY).astype(F32) * 0.125
        ex.append((upper - mx).astype(BF))
        ey.append((py - my).astype(BF))
        oc = geo_ref[i, 2, k : k + 1, :]
        w = wt_ref[i, k : k + 1, :].astype(F32)
        levels = []
        for d in range(LV):
            cw = jnp.zeros((1, TR), F32)
            for o in range(NOC):
                cw = jnp.where(oc == o, cw_ref[o + d], cw)
            levels.append(jnp.broadcast_to(w * cw, (16, TR)).astype(BF))
        wd.append(levels)
    zero16 = jnp.zeros((16, TR), BF)

    def live_of(b, dx, kind):
        i, k = b // 2, b % 2
        base = (dx + 1) * 3
        if kind == 0:
            return ap_ref[i, k, base + 1]
        up = ap_ref[i, k, base + 2]
        down = ap_ref[i, k, base]
        return jnp.where(core == 1, up, down) if kind == 1 else jnp.where(core == 1, down, up)

    def amplitude(slot, dx, kind, nlev):
        shift = {0: 0, 1: step, 2: -step}[kind]
        for b in range(NB):
            gone = (1 - live_of(b, dx, kind)).astype(F32) * 64.0
            dy = jnp.abs(ey[b] + shift.astype(F32).astype(BF) if kind else ey[b]) + gone.astype(BF)
            for g in range(PX // 2):
                dist = jnp.abs(ex[b] + jnp.asarray(2 * dx + 0.25 * g, BF)) + dy
                level = jnp.floor(dist)
                for d in range(nlev):
                    a_ref[slot, 16 * g : 16 * g + 16, d * NJ + b * TR : d * NJ + b * TR + TR] = jnp.where(
                        level == d, wd[b][d], zero16
                    )

    def nlev_of(dx, kind):
        if kind == 0:
            return L_X if dx else L_OWN
        return LV if dx else L_Y

    for k in range(3):
        amplitude(k, *order[k], nlev_of(*order[k]))

    loads[5].wait()
    traces = tr_ref[...]
    for c in range(NC):
        t_ref[c] = jnp.dot(traces, i_ref[c], preferred_element_type=F32).astype(BF)

    for b in range(NB):
        i, k = b // 2, b % 2
        oc_row = jnp.broadcast_to(geo_ref[i, 2, k : k + 1, :], (TR, TR)).astype(F32)
        oc = jnp.transpose(oc_row)
        oc = jnp.concatenate([oc, oc], axis=1).astype(BF)
        for r in range(0, TR, 16):
            o = oc[r : r + 16]
            row = b * TR + r
            b2 = o >= 4
            o = jnp.where(b2, o - 4, o)
            b1 = o >= 2
            o = jnp.where(b1, o - 2, o)
            b0 = o >= 1
            t = [t_ref[c, row : row + 16, :] for c in range(NC)]
            t = [jnp.where(b2, t[c + 4], t[c]) for c in range(NC - 4)]
            t = [jnp.where(b1, t[c + 2], t[c]) for c in range(NC - 6)]
            t = [jnp.where(b0, t[c + 1], t[c]) for c in range(NC - 7)]
            for d in range(LV):
                v_ref[d * NJ + row : d * NJ + row + 16, :] = t[d]

    def migrate(slot, nlev):
        return jnp.dot(a_ref[slot, :, : nlev * NJ], v_ref[: nlev * NJ, :], preferred_element_type=F32)

    for k, n in enumerate(order):
        nlev = nlev_of(*n)
        if k >= 3:
            amplitude(k, *n, nlev)
        sent[k] = migrate(k, nlev).astype(BF)
        if k == 0:
            pl.semaphore_wait(barrier, count)
        guarded(exists(*n), lambda k=k: copies[k].start())

    amplitude(8, 0, 0, L_OWN)
    out_ref[...] = migrate(8, L_OWN).reshape(PX, PY, NT)

    for k in (7, 3, 4, 5, 6, 1, 2, 0):
        dx, kind = order[k]

        def take(k=k):
            copies[k].wait_recv()
            out_ref[...] += got[k].astype(F32).reshape(PX, PY, NT)

        guarded(exists(-dx, kind), take)

    for k, n in enumerate(order):
        guarded(exists(*n), lambda k=k: copies[k].wait_send())


def per_device(traces, aperture, geometry, trace_weight, class_weight, traveltime):
    hbm = pl.BlockSpec(memory_space=pltpu.HBM)
    tile = (PTS, NT)
    return pl.pallas_call(
        kernel,
        out_shape=jax.ShapeDtypeStruct((PX, PY, NT), F32),
        in_specs=[hbm] * 6,
        out_specs=pl.BlockSpec(memory_space=pltpu.VMEM),
        scratch_shapes=[
            pltpu.VMEM((NJ, NS), BF),
            pltpu.SMEM((2, 2, 9), jnp.int32),
            pltpu.VMEM((2, 3, 2, TR), jnp.int32),
            pltpu.VMEM((2, 2, TR), BF),
            pltpu.SMEM((NC,), F32),
            pltpu.VMEM((NC, NT), jnp.int32),
            pltpu.VMEM((NC, NS, NT), BF),
            pltpu.VMEM((NC, NJ, NT), BF),
            pltpu.VMEM((LV * NJ, NT), BF),
            pltpu.VMEM((9, PTS, LV * NJ), BF),
            pltpu.VMEM((8,) + tile, BF),
            pltpu.VMEM((8,) + tile, BF),
            pltpu.SemaphoreType.DMA((6,)),
            pltpu.SemaphoreType.DMA((8,)),
            pltpu.SemaphoreType.DMA((8,)),
        ],
        compiler_params=pltpu.CompilerParams(
            collective_id=0, has_side_effects=True, vmem_limit_bytes=32 * 1024 * 1024
        ),
        cost_estimate=pl.CostEstimate(flops=3_000_000_000, bytes_accessed=2_000_000, transcendentals=0),
        name="migrate",
    )(
        *(
            pltpu.with_memory_space_constraint(x, pltpu.HBM)
            for x in (
                traces.reshape(NJ, NS),
                aperture,
                geometry.transpose(0, 2, 1, 3),
                trace_weight,
                class_weight,
                traveltime,
            )
        )
    )


def solution(mesh):
    return jax.shard_map(
        per_device,
        mesh=mesh,
        in_specs=(
            P("gx", "gy", None, None),
            P("gx", "gy", None),
            P("gx", "gy", None, None),
            P("gx", "gy", None),
            P(),
            P(),
        ),
        out_specs=P("gx", "gy", None),
        check_vma=False,
    )
```

time: 173 us -> 17.1 us (0.10)
  the two profiles are of different devices: /device:TPU:255 before, /device:TPU:264 now
where the time goes in v2:
time: 17.1 us; the launch traced here: 17 us
  Pallas kernels  16.3 us (95%)
  local copies, waits for them, and re-layouts  0.66 us (4%)
    pallas_call x1, Pallas kernels, per_device(): pl.pallas_call(kernel, out_shape=jax.ShapeDtypeStruct((PX, PY, NT), F32),...  16.3 us
    unnamed x1, local copies, waits for them, and re-layouts  0.66 us

profile of v2, /device:TPU:264, one launch (start us, length us, event | category | flops | bytes accessed | tf_op | source)
XLA Modules:
  0.0 17.0 jit_solution(7652830598777394090)
XLA Ops:
  0.0 16.3 %migrate.1 = f32[16,8,256]{2,1,0:T(8,128)S(1)} custom-call(bf16[512,256]{1,0:T(8,128)(2,1)} %bitcast.2, s32[2,2,9]{2,1,0:T(2,128)} %ap_hbm.1, s32[2,3,2,128]{3,2,1,0:T(2,128)} %bitcast.3, bf16[2,2,128]{2,1,0:T(2,128)(2,1)} %wt_hbm.1, f32[14]{0:T(128)} %cw_hbm.1, s32[14,256]{1,0:T(8,128)} %tt_hbm.1), custom_call_target="tpu_custom_call" | custom-call | flops 3000000000 | bytes 2000000 | tf_op jit(solution)/shard_map/migrate/pallas_call | solution.py:209
  16.3 0.7 %copy.8 = f32[16,8,256]{2,1,0:T(8,128)} copy(f32[16,8,256]{2,1,0:T(8,128)S(1)} %migrate.1) | data formatting | bytes 262144

commit v3 on v2

--- a/solution.py
+++ b/solution.py
@@ -24,7 +24,7 @@
 
 def kernel(
     tr_hbm, ap_hbm, geo_hbm, wt_hbm, cw_hbm, tt_hbm, out_ref,
-    tr_ref, ap_ref, geo_ref, wt_ref, cw_ref, tt_ref, i_ref, t_ref, v_ref, a_ref, sent, got, load, send, recv,
+    tr_ref, ap_ref, geo_ref, wt_ref, cw_ref, tt_ref, i_ref, t_ref, v_ref, a_ref, held, sent, got, load, send, recv,
 ):
     gx = lax.axis_index("gx")
     gy = lax.axis_index("gy")
@@ -34,8 +34,13 @@
     step = 2 * core - 1
     has_x = {-1: gx > 0, 1: gx < ngx - 1, 0: None}
     has_far = jnp.logical_and(gy + step >= 0, gy + step < ngy)
-
-    order = [(0, 1), (-1, 1), (1, 1), (-1, 2), (1, 2), (-1, 0), (1, 0), (0, 2)]
+    column = gy // 2
+    rank = lax.rem(column, 4)
+    at_end = jnp.where(core == 1, rank == 3, rank == 0)
+    route = jnp.logical_and(at_end, has_far)
+    early = jnp.logical_or(jnp.logical_and(gx == 0, jnp.logical_and(route, lax.rem(column // 4, 2) == 0)), gx + gy == 1)
+
+    order = [(0, 1), (-1, 1), (1, 1), (-1, 2), (1, 2), (0, 2), (-1, 0), (1, 0)]
 
     def device(dx, kind):
         return (gx + dx, gy + {0: 0, 1: step, 2: -step}[kind])
@@ -52,34 +57,46 @@
         else:
             pl.when(cond)(body)
 
-    barrier = pltpu.get_barrier_semaphore()
-    count = jnp.int32(0)
-    for n in order:
-        cond = exists(*n)
-        guarded(
-            cond,
-            lambda n=n: pl.semaphore_signal(barrier, inc=1, device_id=device(*n), device_id_type=MESH),
-        )
-        count = count + (1 if cond is None else cond.astype(jnp.int32))
-
     loads = [
         pltpu.make_async_copy(src, dst, load.at[k])
         for k, (src, dst) in enumerate(
-            [(tt_hbm, tt_ref), (geo_hbm, geo_ref), (wt_hbm, wt_ref), (cw_hbm, cw_ref), (ap_hbm, ap_ref), (tr_hbm, tr_ref)]
+            [(tt_hbm, tt_ref), (tr_hbm, tr_ref), (geo_hbm, geo_ref), (wt_hbm, wt_ref), (cw_hbm, cw_ref), (ap_hbm, ap_ref)]
         )
     ]
-    for copy in loads:
+    loads[0].start()
+    loads[1].start()
+
+    barrier = pltpu.get_barrier_semaphore()
+    count = jnp.int32(1)
+    greeted = [(0, 1, has_far), (-1, 1, None), (1, 1, None), (-1, 0, has_x[-1]), (1, 0, has_x[1])]
+    for dx, kind, cond in greeted:
+        if cond is None:
+            cond = jnp.logical_and(route, has_x[dx])
+        pl.when(cond)(
+            lambda dx=dx, kind=kind: pl.semaphore_signal(
+                barrier, inc=1, device_id=device(dx, kind), device_id_type=MESH
+            )
+        )
+        count = count + cond.astype(jnp.int32)
+    pl.semaphore_signal(barrier, inc=1, device_id=device(0, 2), device_id_type=MESH)
+
+    for copy in loads[2:]:
         copy.start()
 
     copies = []
     for k, (dx, kind) in enumerate(order):
+        target = device(dx, kind)
+        if dx and kind == 1:
+            target = (jnp.where(at_end, gx + dx, gx), gy + step)
+        elif dx and kind == 2:
+            target = device(0, 2)
         copies.append(
             pltpu.make_async_remote_copy(
                 src_ref=sent.at[k],
                 dst_ref=got.at[k],
                 send_sem=send.at[k],
                 recv_sem=recv.at[k],
-                device_id=device(dx, kind),
+                device_id=target,
                 device_id_type=MESH,
             )
         )
@@ -97,7 +114,7 @@
         w0 = jnp.broadcast_to(1.0 - frac, (NS, NT)).astype(BF)
         i_ref[c] = jnp.where(sample == s0, w0, jnp.where(sample == s1, w1, zero))
 
-    for copy in loads[1:5]:
+    for copy in loads[2:]:
         copy.wait()
     row16 = lax.broadcasted_iota(jnp.int32, (16, TR), 0)
     upper = (row16 // 8).astype(F32) * 0.125
@@ -147,57 +164,103 @@
             return L_X if dx else L_OWN
         return LV if dx else L_Y
 
-    for k in range(3):
-        amplitude(k, *order[k], nlev_of(*order[k]))
-
-    loads[5].wait()
-    traces = tr_ref[...]
-    for c in range(NC):
-        t_ref[c] = jnp.dot(traces, i_ref[c], preferred_element_type=F32).astype(BF)
-
+    loads[1].wait()
+    columns = []
     for b in range(NB):
         i, k = b // 2, b % 2
-        oc_row = jnp.broadcast_to(geo_ref[i, 2, k : k + 1, :], (TR, TR)).astype(F32)
-        oc = jnp.transpose(oc_row)
-        oc = jnp.concatenate([oc, oc], axis=1).astype(BF)
-        for r in range(0, TR, 16):
-            o = oc[r : r + 16]
-            row = b * TR + r
-            b2 = o >= 4
-            o = jnp.where(b2, o - 4, o)
-            b1 = o >= 2
-            o = jnp.where(b1, o - 2, o)
-            b0 = o >= 1
-            t = [t_ref[c, row : row + 16, :] for c in range(NC)]
-            t = [jnp.where(b2, t[c + 4], t[c]) for c in range(NC - 4)]
-            t = [jnp.where(b1, t[c + 2], t[c]) for c in range(NC - 6)]
-            t = [jnp.where(b0, t[c + 1], t[c]) for c in range(NC - 7)]
-            for d in range(LV):
-                v_ref[d * NJ + row : d * NJ + row + 16, :] = t[d]
+        oc = jnp.transpose(jnp.broadcast_to(geo_ref[i, 2, k : k + 1, :], (TR, TR)).astype(F32))
+        columns.append(jnp.concatenate([oc, oc], axis=1).astype(BF))
+
+    def interpolate(c):
+        t_ref[c] = jnp.dot(tr_ref[...], i_ref[c], preferred_element_type=F32).astype(BF)
+
+    def pick(lo, hi):
+        for b in range(NB):
+            for r in range(0, TR, 16):
+                o = columns[b][r : r + 16]
+                row = b * TR + r
+                b2 = o >= 4
+                o = jnp.where(b2, o - 4, o)
+                b1 = o >= 2
+                o = jnp.where(b1, o - 2, o)
+                b0 = o >= 1
+                t = [t_ref[c, row : row + 16, :] for c in range(lo, hi + NOC - 1)]
+                t = [jnp.where(b2, t[c + 4], t[c]) for c in range(len(t) - 4)]
+                t = [jnp.where(b1, t[c + 2], t[c]) for c in range(len(t) - 2)]
+                t = [jnp.where(b0, t[c + 1], t[c]) for c in range(len(t) - 1)]
+                for d in range(lo, hi):
+                    v_ref[d * NJ + row : d * NJ + row + 16, :] = t[d - lo]
 
     def migrate(slot, nlev):
         return jnp.dot(a_ref[slot, :, : nlev * NJ], v_ref[: nlev * NJ, :], preferred_element_type=F32)
 
+    for c in range(L_Y + NOC - 1):
+        interpolate(c)
+    pick(0, L_Y)
+
     for k, n in enumerate(order):
         nlev = nlev_of(*n)
-        if k >= 3:
+        if k == 1:
+            for c in range(L_Y + NOC - 1, NC):
+                interpolate(c)
+            pick(L_Y, LV)
+
+        def make(k=k, n=n, nlev=nlev):
             amplitude(k, *n, nlev)
-        sent[k] = migrate(k, nlev).astype(BF)
-        if k == 0:
-            pl.semaphore_wait(barrier, count)
-        guarded(exists(*n), lambda k=k: copies[k].start())
+            tile = migrate(k, nlev)
+            if k < 6:
+                sent[k] = tile.astype(BF)
+            else:
+                held[k - 6] = tile
+
+        guarded(exists(*n), make)
+        if k < 6:
+
+            @pl.when(jnp.logical_not(early))
+            def _(k=k, n=n):
+                if k == 0:
+                    pl.semaphore_wait(barrier, count)
+                guarded(exists(*n), lambda: copies[k].start())
 
     amplitude(8, 0, 0, L_OWN)
     out_ref[...] = migrate(8, L_OWN).reshape(PX, PY, NT)
 
-    for k in (7, 3, 4, 5, 6, 1, 2, 0):
-        dx, kind = order[k]
-
-        def take(k=k):
-            copies[k].wait_recv()
-            out_ref[...] += got[k].astype(F32).reshape(PX, PY, NT)
-
-        guarded(exists(-dx, kind), take)
+    @pl.when(early)
+    def _():
+        pl.semaphore_wait(barrier, count)
+        for k, n in enumerate(order[:6]):
+            guarded(exists(*n), lambda k=k: copies[k].start())
+
+    def add(k):
+        copies[k].wait_recv()
+        out_ref[...] += got[k].astype(F32).reshape(PX, PY, NT)
+
+    add(5)
+
+    for dx, corner, near, k in ((-1, 1, 3, 6), (1, 2, 4, 7)):
+
+        @pl.when(has_x[dx])
+        def _(corner=corner, near=near, k=k):
+            copies[near].wait_recv()
+            held[k - 6] += got[near].astype(F32)
+
+            @pl.when(jnp.logical_and(has_far, jnp.logical_not(at_end)))
+            def _():
+                copies[corner].wait_recv()
+                held[k - 6] += got[corner].astype(F32)
+
+            sent[k] = held[k - 6].astype(BF)
+            copies[k].start()
+
+    pl.when(jnp.logical_and(has_far, jnp.logical_not(at_end)))(lambda: add(0))
+    pl.when(has_x[1])(lambda: add(6))
+    pl.when(has_x[-1])(lambda: add(7))
+
+    @pl.when(route)
+    def _():
+        add(0)
+        pl.when(has_x[1])(lambda: add(1))
+        pl.when(has_x[-1])(lambda: add(2))
 
     for k, n in enumerate(order):
         guarded(exists(*n), lambda k=k: copies[k].wait_send())
@@ -222,6 +285,7 @@
             pltpu.VMEM((NC, NJ, NT), BF),
             pltpu.VMEM((LV * NJ, NT), BF),
             pltpu.VMEM((9, PTS, LV * NJ), BF),
+            pltpu.VMEM((2,) + tile, F32),
             pltpu.VMEM((8,) + tile, BF),
             pltpu.VMEM((8,) + tile, BF),
             pltpu.SemaphoreType.DMA((6,)),

time: 17.1 us -> 16.4 us (0.959)
  the two profiles are of different devices: /device:TPU:264 before, /device:TPU:255 now
where the time goes in v3:
time: 16.4 us; the launch traced here: 16.2 us
  Pallas kernels  15.6 us (95%)
  local copies, waits for them, and re-layouts  0.66 us (4%)
    pallas_call x1, Pallas kernels, per_device(): pl.pallas_call(kernel, out_shape=jax.ShapeDtypeStruct((PX, PY, NT), F32),...  15.6 us
    unnamed x1, local copies, waits for them, and re-layouts  0.66 us

profile of v3, /device:TPU:255, one launch (start us, length us, event | category | flops | bytes accessed | tf_op | source)
XLA Modules:
  0.0 16.2 jit_solution(3465202067501272946)
XLA Ops:
  0.0 15.6 %migrate.1 = f32[16,8,256]{2,1,0:T(8,128)S(1)} custom-call(bf16[512,256]{1,0:T(8,128)(2,1)} %bitcast.2, s32[2,2,9]{2,1,0:T(2,128)} %ap_hbm.1, s32[2,3,2,128]{3,2,1,0:T(2,128)} %bitcast.3, bf16[2,2,128]{2,1,0:T(2,128)(2,1)} %wt_hbm.1, f32[14]{0:T(128)} %cw_hbm.1, s32[14,256]{1,0:T(8,128)} %tt_hbm.1), custom_call_target="tpu_custom_call" | custom-call | flops 3000000000 | bytes 2000000 | tf_op jit(solution)/shard_map/migrate/pallas_call | solution.py:272
  15.6 0.7 %copy.8 = f32[16,8,256]{2,1,0:T(8,128)} copy(f32[16,8,256]{2,1,0:T(8,128)S(1)} %migrate.1) | data formatting | bytes 262144

commit v4 on v3

--- a/solution.py
+++ b/solution.py
@@ -24,7 +24,7 @@
 
 def kernel(
     tr_hbm, ap_hbm, geo_hbm, wt_hbm, cw_hbm, tt_hbm, out_ref,
-    tr_ref, ap_ref, geo_ref, wt_ref, cw_ref, tt_ref, i_ref, t_ref, v_ref, a_ref, held, sent, got, load, send, recv,
+    tr_ref, ap_ref, geo_ref, wt_ref, cw_ref, tt_ref, i_ref, t_ref, v_ref, a_ref, held, sent, got, load, send, recv, near_sem,
 ):
     gx = lax.axis_index("gx")
     gy = lax.axis_index("gy")
@@ -38,7 +38,19 @@
     rank = lax.rem(column, 4)
     at_end = jnp.where(core == 1, rank == 3, rank == 0)
     route = jnp.logical_and(at_end, has_far)
-    early = jnp.logical_or(jnp.logical_and(gx == 0, jnp.logical_and(route, lax.rem(column // 4, 2) == 0)), gx + gy == 1)
+    near_half = lax.rem(column // 4, 2) == 0
+    partner_at_end = jnp.where(core == 1, rank == 0, rank == 3)
+    partner_far = gy - 2 * step
+    beside_route = jnp.logical_and(partner_at_end, jnp.logical_and(partner_far >= 0, partner_far < ngy))
+    bend = column // 8 == 3
+    late = jnp.logical_and(route, jnp.logical_and(near_half, gx == 0))
+    inner = jnp.logical_and(route, jnp.logical_and(near_half, gx == 1))
+    early = gx + gy == 1
+    quick = jnp.logical_and(jnp.logical_not(early), jnp.logical_or(jnp.logical_not(route), jnp.logical_and(jnp.logical_and(gx < 2, jnp.logical_not(bend)), jnp.logical_not(near_half))))
+    middle = jnp.logical_and(route, jnp.logical_not(jnp.logical_or(inner, jnp.logical_or(quick, late))))
+    origin = gx + gy == 0
+    beside = jnp.logical_and(gx == 0, gy == 1)
+    across = jnp.logical_and(gx == 1, gy == 1)
 
     order = [(0, 1), (-1, 1), (1, 1), (-1, 2), (1, 2), (0, 2), (-1, 0), (1, 0)]
 
@@ -67,18 +79,27 @@
     loads[1].start()
 
     barrier = pltpu.get_barrier_semaphore()
-    count = jnp.int32(1)
-    greeted = [(0, 1, has_far), (-1, 1, None), (1, 1, None), (-1, 0, has_x[-1]), (1, 0, has_x[1])]
-    for dx, kind, cond in greeted:
-        if cond is None:
-            cond = jnp.logical_and(route, has_x[dx])
+    off_route = jnp.logical_not(route)
+
+    def greet(cond, dx, kind):
         pl.when(cond)(
-            lambda dx=dx, kind=kind: pl.semaphore_signal(
-                barrier, inc=1, device_id=device(dx, kind), device_id_type=MESH
-            )
-        )
-        count = count + cond.astype(jnp.int32)
-    pl.semaphore_signal(barrier, inc=1, device_id=device(0, 2), device_id_type=MESH)
+            lambda: pl.semaphore_signal(barrier, inc=1, device_id=device(dx, kind), device_id_type=MESH)
+        )
+
+    greet(has_far, 0, 1)
+    for dx in (-1, 1):
+        greet(jnp.logical_and(route, has_x[dx]), dx, 1)
+        greet(jnp.logical_and(off_route, has_x[dx]), dx, 0)
+        greet(jnp.logical_and(route, has_x[dx]), dx, 2)
+    greet(jnp.logical_not(beside_route), 0, 2)
+    sides = has_x[-1].astype(jnp.int32) + has_x[1].astype(jnp.int32)
+    count = jnp.where(
+        route, 1 + sides, 1 + has_far.astype(jnp.int32) + sides + jnp.where(beside_route, sides, 0)
+    )
+    pl.when(across)(
+        lambda: pl.semaphore_signal(barrier, inc=1, device_id=(gx - 1, gy - 1), device_id_type=MESH)
+    )
+    count = count + origin.astype(jnp.int32)
 
     for copy in loads[2:]:
         copy.start()
@@ -100,6 +121,17 @@
                 device_id_type=MESH,
             )
         )
+
+    copies.append(
+        pltpu.make_async_remote_copy(
+            src_ref=sent.at[4],
+            dst_ref=got.at[8],
+            send_sem=send.at[8],
+            recv_sem=recv.at[8],
+            device_id=(gx + 1, gy + 1),
+            device_id_type=MESH,
+        )
+    )
 
     loads[0].wait()
     sample = lax.broadcasted_iota(jnp.int32, (NS, NT), 0).astype(F32).astype(BF)
@@ -198,63 +230,119 @@
         interpolate(c)
     pick(0, L_Y)
 
-    for k, n in enumerate(order):
-        nlev = nlev_of(*n)
-        if k == 1:
-            for c in range(L_Y + NOC - 1, NC):
-                interpolate(c)
-            pick(L_Y, LV)
-
-        def make(k=k, n=n, nlev=nlev):
-            amplitude(k, *n, nlev)
+    def make(k):
+        dx, kind = order[k]
+        nlev = nlev_of(dx, kind)
+
+        def body():
+            amplitude(k, dx, kind, nlev)
             tile = migrate(k, nlev)
             if k < 6:
                 sent[k] = tile.astype(BF)
             else:
                 held[k - 6] = tile
 
-        guarded(exists(*n), make)
-        if k < 6:
-
-            @pl.when(jnp.logical_not(early))
-            def _(k=k, n=n):
-                if k == 0:
-                    pl.semaphore_wait(barrier, count)
-                guarded(exists(*n), lambda: copies[k].start())
-
-    amplitude(8, 0, 0, L_OWN)
-    out_ref[...] = migrate(8, L_OWN).reshape(PX, PY, NT)
+        guarded(exists(dx, kind), body)
+
+    def start(*slots):
+        for k in slots:
+            cond = exists(*order[k])
+            if k == 4:
+                pl.when(origin)(lambda: copies[8].start())
+                cond = jnp.logical_and(cond, jnp.logical_not(origin))
+            guarded(cond, lambda k=k: copies[k].start())
+
+    def own():
+        amplitude(8, 0, 0, L_OWN)
+        out_ref[...] = migrate(8, L_OWN).reshape(PX, PY, NT)
+
+    def meet():
+        pl.semaphore_wait(barrier, count)
+        pl.when(beside_route)(
+            lambda: pl.semaphore_signal(near_sem, inc=1, device_id=device(0, 2), device_id_type=MESH)
+        )
+
+    make(0)
+
+    @pl.when(quick)
+    def _():
+        meet()
+        start(0)
+
+    for c in range(L_Y + NOC - 1, NC):
+        interpolate(c)
+    pick(L_Y, LV)
+    make(1)
+    make(2)
+
+    def start_far():
+        low = gx < 2
+        pl.when(low)(lambda: start(2))
+        pl.when(jnp.logical_not(low))(lambda: start(1))
+        start(0)
+        pl.when(low)(lambda: start(1))
+        pl.when(jnp.logical_not(low))(lambda: start(2))
+
+    @pl.when(middle)
+    def _():
+        meet()
+        start_far()
+
+    pl.when(quick)(lambda: start(1, 2))
+    make(3)
+    make(4)
+    make(5)
+    pl.when(route)(lambda: pl.semaphore_wait(near_sem, 1))
+    pl.when(jnp.logical_not(early))(lambda: start(3, 4, 5))
+    make(6)
+    make(7)
+
+    @pl.when(inner)
+    def _():
+        meet()
+        start_far()
 
     @pl.when(early)
     def _():
-        pl.semaphore_wait(barrier, count)
-        for k, n in enumerate(order[:6]):
-            guarded(exists(*n), lambda k=k: copies[k].start())
+        own()
+        meet()
+        start(0, 1, 2, 3, 4, 5)
+
+    off_far = jnp.logical_and(has_far, jnp.logical_not(at_end))
+
+    for dx, corner, near, k in ((-1, 1, 3, 6), (1, 2, 4, 7)):
+
+        @pl.when(has_x[dx])
+        def _(corner=corner, near=near, k=k):
+            @pl.when(jnp.logical_not(beside))
+            def _():
+                copies[near].wait_recv()
+                held[k - 6] += got[near].astype(F32)
+
+            @pl.when(off_far)
+            def _():
+                copies[corner].wait_recv()
+                held[k - 6] += got[corner].astype(F32)
+
+            sent[k] = held[k - 6].astype(BF)
+            copies[k].start()
+
+    pl.when(jnp.logical_not(early))(own)
+
+    @pl.when(late)
+    def _():
+        meet()
+        start_far()
 
     def add(k):
         copies[k].wait_recv()
         out_ref[...] += got[k].astype(F32).reshape(PX, PY, NT)
 
     add(5)
-
-    for dx, corner, near, k in ((-1, 1, 3, 6), (1, 2, 4, 7)):
-
-        @pl.when(has_x[dx])
-        def _(corner=corner, near=near, k=k):
-            copies[near].wait_recv()
-            held[k - 6] += got[near].astype(F32)
-
-            @pl.when(jnp.logical_and(has_far, jnp.logical_not(at_end)))
-            def _():
-                copies[corner].wait_recv()
-                held[k - 6] += got[corner].astype(F32)
-
-            sent[k] = held[k - 6].astype(BF)
-            copies[k].start()
-
-    pl.when(jnp.logical_and(has_far, jnp.logical_not(at_end)))(lambda: add(0))
+    pl.when(off_far)(lambda: add(0))
     pl.when(has_x[1])(lambda: add(6))
     pl.when(has_x[-1])(lambda: add(7))
+    pl.when(across)(lambda: add(8))
 
     @pl.when(route)
     def _():
@@ -263,7 +351,11 @@
         pl.when(has_x[-1])(lambda: add(2))
 
     for k, n in enumerate(order):
-        guarded(exists(*n), lambda k=k: copies[k].wait_send())
+        cond = exists(*n)
+        if k == 4:
+            pl.when(origin)(lambda: copies[8].wait_send())
+            cond = jnp.logical_and(cond, jnp.logical_not(origin))
+        guarded(cond, lambda k=k: copies[k].wait_send())
 
 
 def per_device(traces, aperture, geometry, trace_weight, class_weight, traveltime):
@@ -287,10 +379,11 @@
             pltpu.VMEM((9, PTS, LV * NJ), BF),
             pltpu.VMEM((2,) + tile, F32),
             pltpu.VMEM((8,) + tile, BF),
-            pltpu.VMEM((8,) + tile, BF),
+            pltpu.VMEM((9,) + tile, BF),
             pltpu.SemaphoreType.DMA((6,)),
-            pltpu.SemaphoreType.DMA((8,)),
-            pltpu.SemaphoreType.DMA((8,)),
+            pltpu.SemaphoreType.DMA((9,)),
+            pltpu.SemaphoreType.DMA((9,)),
+            pltpu.SemaphoreType.REGULAR,
         ],
         compiler_params=pltpu.CompilerParams(
             collective_id=0, has_side_effects=True, vmem_limit_bytes=32 * 1024 * 1024

time: 16.4 us -> 16.7 us (1.018)
  the two profiles are of different devices: /device:TPU:255 before, /device:TPU:239 now
where the time goes in v4:
time: 16.7 us; the launch traced here: 16.5 us
  Pallas kernels  15.8 us (95%)
  local copies, waits for them, and re-layouts  0.66 us (4%)
    pallas_call x1, Pallas kernels, per_device(): pl.pallas_call(kernel, out_shape=jax.ShapeDtypeStruct((PX, PY, NT), F32),...  15.8 us
    unnamed x1, local copies, waits for them, and re-layouts  0.66 us

profile of v4, /device:TPU:239, one launch (start us, length us, event | category | flops | bytes accessed | tf_op | source)
XLA Modules:
  0.0 16.5 jit_solution(183252490685830101)
XLA Ops:
  0.0 15.8 %migrate.1 = f32[16,8,256]{2,1,0:T(8,128)S(1)} custom-call(bf16[512,256]{1,0:T(8,128)(2,1)} %bitcast.2, s32[2,2,9]{2,1,0:T(2,128)} %ap_hbm.1, s32[2,3,2,128]{3,2,1,0:T(2,128)} %bitcast.3, bf16[2,2,128]{2,1,0:T(2,128)(2,1)} %wt_hbm.1, f32[14]{0:T(128)} %cw_hbm.1, s32[14,256]{1,0:T(8,128)} %tt_hbm.1), custom_call_target="tpu_custom_call" | custom-call | flops 3000000000 | bytes 2000000 | tf_op jit(solution)/shard_map/migrate/pallas_call | solution.py:364
  15.8 0.7 %copy.8 = f32[16,8,256]{2,1,0:T(8,128)} copy(f32[16,8,256]{2,1,0:T(8,128)S(1)} %migrate.1) | data formatting | bytes 262144

commit v5 on v4

--- a/solution.py
+++ b/solution.py
@@ -44,9 +44,9 @@
     beside_route = jnp.logical_and(partner_at_end, jnp.logical_and(partner_far >= 0, partner_far < ngy))
     bend = column // 8 == 3
     late = jnp.logical_and(route, jnp.logical_and(near_half, gx == 0))
-    inner = jnp.logical_and(route, jnp.logical_and(near_half, gx == 1))
+    inner = gx < 0
     early = gx + gy == 1
-    quick = jnp.logical_and(jnp.logical_not(early), jnp.logical_or(jnp.logical_not(route), jnp.logical_and(jnp.logical_and(gx < 2, jnp.logical_not(bend)), jnp.logical_not(near_half))))
+    quick = jnp.logical_and(jnp.logical_not(early), jnp.logical_not(late))
     middle = jnp.logical_and(route, jnp.logical_not(jnp.logical_or(inner, jnp.logical_or(quick, late))))
     origin = gx + gy == 0
     beside = jnp.logical_and(gx == 0, gy == 1)
@@ -276,12 +276,12 @@
     make(2)
 
     def start_far():
-        low = gx < 2
-        pl.when(low)(lambda: start(2))
-        pl.when(jnp.logical_not(low))(lambda: start(1))
-        start(0)
-        pl.when(low)(lambda: start(1))
-        pl.when(jnp.logical_not(low))(lambda: start(2))
+        pl.when(gx == 1)(lambda: start(0))
+        pl.when(gx < 2)(lambda: start(2))
+        pl.when(gx >= 2)(lambda: start(1))
+        pl.when(gx != 1)(lambda: start(0))
+        pl.when(gx < 2)(lambda: start(1))
+        pl.when(gx >= 2)(lambda: start(2))
 
     @pl.when(middle)
     def _():

time: 16.7 us -> 16.4 us (0.982)
  the two profiles are of different devices: /device:TPU:239 before, /device:TPU:255 now
where the time goes in v5:
time: 16.4 us; the launch traced here: 16.3 us
  Pallas kernels  15.6 us (95%)
  local copies, waits for them, and re-layouts  0.66 us (4%)
    pallas_call x1, Pallas kernels, per_device(): pl.pallas_call(kernel, out_shape=jax.ShapeDtypeStruct((PX, PY, NT), F32),...  15.6 us
    unnamed x1, local copies, waits for them, and re-layouts  0.66 us

profile of v5, /device:TPU:255, one launch (start us, length us, event | category | flops | bytes accessed | tf_op | source)
XLA Modules:
  0.0 16.3 jit_solution(9418760402566965943)
XLA Ops:
  0.0 15.6 %migrate.1 = f32[16,8,256]{2,1,0:T(8,128)S(1)} custom-call(bf16[512,256]{1,0:T(8,128)(2,1)} %bitcast.2, s32[2,2,9]{2,1,0:T(2,128)} %ap_hbm.1, s32[2,3,2,128]{3,2,1,0:T(2,128)} %bitcast.3, bf16[2,2,128]{2,1,0:T(2,128)(2,1)} %wt_hbm.1, f32[14]{0:T(128)} %cw_hbm.1, s32[14,256]{1,0:T(8,128)} %tt_hbm.1), custom_call_target="tpu_custom_call" | custom-call | flops 3000000000 | bytes 2000000 | tf_op jit(solution)/shard_map/migrate/pallas_call | solution.py:364
  15.6 0.7 %copy.8 = f32[16,8,256]{2,1,0:T(8,128)} copy(f32[16,8,256]{2,1,0:T(8,128)S(1)} %migrate.1) | data formatting | bytes 262144
